TPU v7x, 32 devices: a 4x4x1 block of a 4x4x8 slice. The times are simulated.
32 devices in a mesh: grp: 1 (over z), dz: 4 (over y), dy: 4 (over x), dx: 2 (over core).
Axes of the slice: x: 4, y: 4, z: 1, core: 2. Of those that a mesh axis runs over, the one named last changes fastest.
The devices are a block of a 4x4x8 slice.
Arguments:
- x_in: bfloat16 [6144, 7168], P(('grp', 'dx', 'dz'), 'dy')
- w_gate: bfloat16 [7168, 20480], P('dy', ('dz', 'dx'))
- w_up: bfloat16 [7168, 20480], P('dy', ('dz', 'dx'))
- w_down: bfloat16 [20480, 7168], P('dz', ('dy', 'dx'))
Outputs:
- output: bfloat16 [6144, 7168], P(('grp', 'dx', 'dz'), 'dy')
All inputs are finite; a program needn't handle non-finite values.
Results may differ from a plain program's by a relative error of at most 0.0124762.
Values are sent between devices in bfloat16 or wider.
A program may use at most 768 MiB of HBM per device.

v0:
```python
import jax
import jax.numpy as jnp
from jax import lax
from jax.experimental import pallas as pl
from jax.experimental.pallas import tpu as pltpu
from jax.sharding import PartitionSpec as P

MESH = pl.DeviceIdType.MESH
RING = 4
H_SLOTS = 7
Z_SLOTS = 6
AHEAD, AHEAD_LAST = 3, 2
WD_SLOTS = 3
XL, XS, XF, YL, YS, YF, WN, W2, WF, WL, SW, SD, YH, P1 = 0, 2, 3, 5, 9, 13, 17, 21, 25, 29, 33, 49, 50, 52
JOINT = (
    (XF, XF + 1), (YH, YH + 1), tuple(range(YS, YF)), tuple(range(YF, WN)), (WN, WN + 1), (WN + 2, WN + 3), (WF, WF + 1),
    tuple(SW + 4 * j + u for j in range(RING) for u in range(2)), tuple(SW + 4 * j + 2 + u for j in range(RING) for u in range(2)),
)
RECV = {}
for _i in range(P1):
    _group = next((g for g in JOINT if _i in g), (_i,))
    RECV[_i] = RECV[_group[0]] if _i != _group[0] else len(set(RECV.values()))
N_RECV = len(set(RECV.values()))


def _tile(extent, most):
    return next(t for t in range(most, 0, -128) if extent % t == 0)


def _kernel(x_in, wg_in, wu_in, wd_in, z_half, z_part, xg, wgu, ws, hg, wds, wd, zin,
            xbuf, wbuf, hz, wdbuf, zinb, zout, zacc, ofin, hout,
            p1s, p1r, bin_s, bout_s, xsem, wsem, hzsem, wdsem, zinsem, osem,
            os, olr, fs, hr, hws, zs, zr):
    rows, kb = x_in.shape
    hc = wg_in.shape[1] // RING
    nloc = wg_in.shape[1]
    hq = 2 * hc
    mc = wd_in.shape[1]
    part_rows, tn = hout.shape[2:]
    zn = zout.shape[2]
    nt = hq // tn
    nz = 2 * mc // zn
    ng = RING * nt
    ni = 2 * ng
    zstart = nt + 2
    early = (nt + 1) // 2
    pc = (early * tn // 2, hc - early * tn // 2)
    p_src, p_dst = (0, pc[0]), (0, 2 * pc[0])

    b = lax.axis_index("dz")
    a = lax.axis_index("dy")
    c = lax.axis_index("dx")
    step = 1 - 2 * c
    al = lax.rem(a + step + RING, RING)
    ash = lax.rem(a - step + RING, RING)
    a2 = lax.rem(a + 2, RING)
    bl = lax.rem(b + step + RING, RING)
    bsh = lax.rem(b - step + RING, RING)
    xl, xs_ = {"dy": al}, {"dy": ash}
    yl, ys_ = {"dz": bl}, {"dz": bsh}
    sib = {"dx": 1 - c}
    kbs = (a, ash, al, a2)
    w_in = (wg_in, wu_in)

    def dest(s):
        return lax.rem(b - step * (1 + s) + 2 * RING, RING)

    def rc(src, dst, ss, rs, dev):
        return pltpu.make_async_remote_copy(src_ref=src, dst_ref=dst, send_sem=ss, recv_sem=rs, device_id=dev, device_id_type=MESH)

    def lanes(i, n):
        return pl.ds(pl.multiple_of(i * n, 128), n)

    def krows(k):
        return pl.ds(pl.multiple_of(k * kb, 16), kb)

    half = rows // 2

    def w_piece(u, p, q):
        return w_in[u].at[:, pl.ds(pl.multiple_of(q * hc + p_src[p], 128), pc[p])]

    def w_place(u, p, k):
        return wgu.at[u, krows(k), pl.ds(pl.multiple_of(p_dst[p] + c * pc[p], 128), pc[p])]

    def p1(i):
        kind = 0 if i < YL else 1 if i < WN or i >= YH else 2 if i < SW else 3 if i < SD else 4
        sem = (p1s.at[kind], p1r.at[RECV[i]])
        if i >= YH:
            r = pl.ds((i - YH) * half, half)
            return rc(xg.at[b, ash, r], xg.at[b, ash, r], *sem, yl)
        if i < XS:
            r = pl.ds((i - XL) * half, half)
            return rc(x_in.at[r], xg.at[b, a, r], *sem, xl)
        if i < XF:
            return rc(x_in, xg.at[b, a], *sem, xs_)
        if i < YL:
            r = pl.ds((i - XF) * half, half)
            return rc(xg.at[b, ash, r], xg.at[b, ash, r], *sem, xl)
        if i < YF:
            j = (i - YL) % RING
            src = x_in if j == 0 else xg.at[b, kbs[j]]
            return rc(src, xg.at[b, kbs[j]], *sem, yl if i < YS else ys_)
        if i < WN:
            j = i - YF
            return rc(xg.at[bsh, kbs[j]], xg.at[bsh, kbs[j]], *sem, yl)
        if i < WF:
            u, p = (i - WN) % 2, (i - WN) % 4 // 2
            if i < W2:
                return rc(w_piece(u, p, ash), w_place(u, p, a), *sem, xs_)
            return rc(w_piece(u, p, a2), ws.at[u, :, pl.ds(p_src[p], pc[p])], *sem, xl)
        if i < WL:
            u, p = (i - WF) % 2, (i - WF) // 2
            return rc(ws.at[u, :, pl.ds(p_src[p], pc[p])], w_place(u, p, ash), *sem, xl)
        if i < SW:
            u, p = (i - WL) % 2, (i - WL) // 2
            return rc(w_piece(u, p, al), w_place(u, p, a), *sem, xl)
        if i < SD:
            j, p, u = (i - SW) // 4, (i - SW) % 4 // 2, (i - SW) % 2
            dst = w_place(u, p, kbs[j])
            return rc(w_piece(u, p, a) if j == 0 else dst, dst, *sem, sib)
        return rc(wd_in, wds, *sem, sib)

    def go(*idx):
        for i in idx:
            p1(i).start()

    def got(*idx):
        for i in idx:
            with jax.named_scope(f"got{i}"):
                p1(i).wait_recv()

    def total(ref, sem):
        pltpu.make_async_copy(ref, ref, sem).wait()

    def got_all(first, ref):
        with jax.named_scope(f"got{first}"):
            total(ref, p1r.at[RECV[first]])

    def part_of(u_refs, p):
        return u_refs.at[:, :, pl.ds(p_src[p], pc[p])]

    def all_sent():
        quarter = wgu.at[:, :, pl.ds(0, hc)]
        for kind, ref in enumerate((xg.at[0, pl.ds(0, 3)], xg.at[pl.ds(0, 3)], quarter, quarter, wds)):
            total(ref, p1s.at[kind])

    barrier = pltpu.get_barrier_semaphore()
    for dev in (xl, xs_, yl, ys_, sib):
        pl.semaphore_signal(barrier, inc=1, device_id=dev, device_id_type=MESH)
    with jax.named_scope("barrier"):
        pl.semaphore_wait(barrier, 5)

    go(XL, XL + 1, XS, YL, YS, SD, SW, SW + 1, SW + 2, SW + 3, WN, WN + 1)

    def bounce(*classes):
        for i, (size, moves) in enumerate(classes):
            for src, mid, _ in moves:
                pltpu.make_async_copy(src, mid, bin_s.at[i]).start()
        for i, (size, moves) in enumerate(classes):
            total(size, bin_s.at[i])
            for _, _, parts in moves:
                for piece, dst in parts:
                    pltpu.make_async_copy(piece, dst, bout_s.at[i]).start()
        for i, (size, moves) in enumerate(classes):
            total(size, bout_s.at[i])

    def w_down_moves(src, core):
        moves = []
        for cc in range(2):
            for k in range(RING):
                cols = pl.ds((cc * RING + k) * mc, mc)
                parts = []
                for p in range(2):
                    at, end = p_dst[p] + cc * pc[p], p_dst[p] + (cc + 1) * pc[p]
                    while at < end:
                        n = min(end, (at // tn + 1) * tn) - at
                        row = p_src[p] + at - p_dst[p] - cc * pc[p]
                        dst = wd.at[pl.ds((at // tn * RING + k) * tn + at % tn, n), lanes(core, mc)]
                        parts.append((xbuf.at[1, pl.ds(row, n), cols], dst))
                        at += n
                moves.append((src.at[pl.ds(cc * nloc + k * hc, hc)], xbuf.at[1, pl.ds(0, hc), cols], parts))
        return moves

    x_moves = [(x_in, xbuf.at[0, :, pl.ds(0, kb)], [(xbuf.at[0, :, pl.ds(0, kb)], xg.at[b, a])])]
    w_moves, col = [], kb
    for u in range(2):
        for r0 in range(0, kb, rows):
            n = min(rows, kb - r0)
            parts = []
            for p in range(2):
                dst = wgu.at[u, pl.ds(pl.multiple_of(a * kb + r0, 16), n), pl.ds(pl.multiple_of(p_dst[p] + c * pc[p], 128), pc[p])]
                parts.append((xbuf.at[0, pl.ds(0, n), pl.ds(col + p_src[p], pc[p])], dst))
            w_moves.append((w_in[u].at[pl.ds(r0, n), lanes(a, hc)], xbuf.at[0, pl.ds(0, n), pl.ds(col, hc)], parts))
            col += hc
    with jax.named_scope("bounce"):
        bounce((x_in, x_moves), (ws, w_moves), (wd_in, w_down_moves(wd_in, c)))
        zinb[...] = jnp.zeros_like(zinb)

    got(XL)
    go(XF, YH)
    got(XL + 1)
    go(XF + 1, W2, W2 + 1, YH + 1)
    got(XS)
    go(YL + 2, WN + 2, WN + 3)
    got(YL)
    go(YF)
    got_all(XF, xg.at[0, 0])
    go(YL + 3, WL)
    got_all(YH, xg.at[0, 0])
    go(YF + 1)
    got(SD)
    with jax.named_scope("bounce"):
        bounce((wds, w_down_moves(wds, 1 - c)))
    got(W2)
    go(WF)
    got(W2 + 1)
    go(WF + 1, WL + 1, W2 + 2, W2 + 3)
    got(YL + 2)
    go(YF + 2)
    got_all(WN, part_of(ws, 0))
    go(SW + 8, SW + 9)
    got(YL + 3)
    go(YF + 3)
    got(WL)
    go(SW + 4)
    got_all(WF, part_of(ws, 0))
    go(SW + 12, SW + 13)
    got(WL + 1)
    go(SW + 5, WL + 2, YS + 1)
    got(W2 + 2)
    go(WF + 2)
    got(W2 + 3)
    go(WF + 3, WL + 3)

    def x_load(s, k):
        return pltpu.make_async_copy(xg.at[dest(s), k], xbuf.at[lax.rem(s, 2), :, pl.ds(k * kb, kb)], xsem.at[lax.rem(s, 2)])

    def w_load(g, u):
        slot = lax.rem(g, 2)
        return pltpu.make_async_copy(wgu.at[u, :, lanes(lax.rem(g, nt), tn)], wbuf.at[slot, :, pl.ds(u * tn, tn)], wsem.at[slot])

    assert nt >= 4
    nsum = 2 * (RING - 1) * nz
    ta, first_q, last_q = nt - 2, 2 * RING - 2, 2 * RING - 1
    spans = ((0, nt), (0, ta), (ta, nt), (0, ta - 1), (ta - 1, ta))
    wd_rows = [pl.ds(lo * RING * tn, (hi - lo) * RING * tn) for lo, hi in spans]


    def wd_load(w, kind):
        slot = lax.rem(w, WD_SLOTS)
        return pltpu.make_async_copy(wd.at[wd_rows[kind], lanes(lax.rem(w, nz), zn)], wdbuf.at[slot, wd_rows[kind]], wdsem.at[slot])

    def wd_fetch(w):
        for kind in range(5):
            lo, hi = (nsum + (kind - 1) * nz, nsum + kind * nz) if kind else (0, nsum)

            @pl.when((w >= lo) & (w < hi))
            def _():
                wd_load(w, kind).start()

    def zin_load(z, slot):
        return pltpu.make_async_copy(zin.at[z // nz - 2, lax.rem(z, nz)], zinb.at[slot], zinsem.at[slot])

    def pairs(s):
        return jnp.maximum(early - s, 0)

    def item_of(s, h, t):
        m = pairs(s)
        return 2 * nt * s + jnp.where(t < m, 2 * t + h, 2 * m + h * (nt - m) + t - m)

    def place_of(i):
        s, v = i // (2 * nt), lax.rem(i, 2 * nt)
        m = pairs(s)
        w = jnp.maximum(v - 2 * m, 0)
        late = jnp.where(w >= nt - m, 1, 0)
        h = jnp.where(v < 2 * m, lax.rem(v, 2), late)
        t = jnp.where(v < 2 * m, v // 2, m + w - late * (nt - m))
        return s, h, t

    def h_write(g):
        slot = lax.rem(g, H_SLOTS)
        return pltpu.make_async_copy(hout.at[slot], hg.at[dest(g // nt), a, :, lax.rem(g, nt)], hws.at[lax.rem(g, 2)])

    def half_of(s, h, t):
        q = 2 * s + h
        first = jnp.where((q == first_q) & (t >= ta), 1, 0)
        last = jnp.where(q == last_q, 1 + jnp.where(t >= ta - 1, 1, 0) + jnp.where(t >= ta, 1, 0), 0)
        return q + first + last

    def h_long(i):
        s, h, t = place_of(i)
        return rc(hout.at[lax.rem(s * nt + t, H_SLOTS), h], hg.at[dest(s), a, h, t], os.at[lax.rem(i, 8)], olr.at[i], xl)

    def h_short(i):
        s, h, t = place_of(i)
        return rc(hout.at[lax.rem(s * nt + t, H_SLOTS), h], hg.at[dest(s), a, h, t], os.at[lax.rem(i, 8)], hr.at[half_of(s, h, t)], xs_)

    def h_fwd(i):
        s, h, t = place_of(i)
        blk = hg.at[dest(s), ash, h, t]
        return rc(blk, blk, fs.at[lax.rem(i, 8)], hr.at[half_of(s, h, t)], xl)

    def ready(tiles):
        s, r = tiles // nt, lax.rem(tiles, nt)
        m = pairs(s)
        return 2 * nt * s + jnp.where(r <= m, 2 * r, m + r)

    cut = ni - 12

    def issued(forwards, tiles):
        ahead = jnp.where(forwards < cut, forwards + AHEAD, jnp.maximum(forwards + AHEAD_LAST, cut + AHEAD - 1))
        return jnp.minimum(ahead, ready(tiles))

    def send(lo, hi):
        def one(i, carry):
            h_long(i).start()
            h_short(i).start()
            return carry

        lax.fori_loop(lo, hi, one, 0)

    def forwards(g):
        return jnp.where(g < early, 0, jnp.minimum(jnp.maximum(early, 2 * (g - early) + 2), ni))

    def serve(j, tiles):
        h_long(j).wait_recv()
        h_fwd(j).start()
        send(issued(j, tiles), issued(j + 1, tiles))

        @pl.when(j >= 2)
        def _():
            total(hout.at[0], os.at[lax.rem(j - 2, 8)])

        @pl.when(j >= 4)
        def _():
            h_fwd(j - 4).wait_send()

    def pull(q, sem, lo, hi):
        s, h = q // 2, lax.rem(q, 2)
        total(hg.at[0, 0, :, pl.ds(lo, hi - lo)], hr.at[sem])

        def one(t, carry):
            for k in range(RING):
                pltpu.make_async_copy(hg.at[dest(s), k, h, t], hz.at[lax.rem(q, 2), :, lanes(t * RING + k, tn)], hzsem.at[0]).start()
            return carry

        lax.fori_loop(lo, hi, one, 0)

    def pulled(q, lo, hi):
        total(hz.at[lax.rem(q, 2), :, pl.ds(lo * RING * tn, (hi - lo) * RING * tn)], hzsem.at[0])

    def z_send(z):
        slot = lax.rem(z, Z_SLOTS)
        return rc(zout.at[slot], zin.at[z // nz, lax.rem(z, nz)], zs.at[slot], zr.at[z // nz], yl)

    def o_write(z, slot):
        return pltpu.make_async_copy(ofin.at[slot], z_half.at[:, lanes(lax.rem(z, nz), zn)], osem.at[slot])

    def start_w(g):
        w_load(g, 0).start()
        w_load(g, 1).start()

    for k in range(RING):
        x_load(0, k).start()
    got_all(SW, wgu.at[:, :, pl.ds(p_dst[0], pc[0])])
    start_w(0)

    def z_tile(z, carry):
        q, wslot = z // nz, lax.rem(z, WD_SLOTS)
        wd_fetch(z + 2)

        @pl.when(lax.rem(z, nz) == 0)
        def _():
            with jax.named_scope("zinrecv"):
                @pl.when(q >= 2)
                def _():
                    total(zin.at[0], zr.at[q - 2])
                    for y in range(2):
                        zin_load(z + y, lax.rem(z + y, 3)).start()

            with jax.named_scope("harr"):
                pull(q, q, 0, nt)
            with jax.named_scope("hzload"):
                pulled(q, 0, nt)

        @pl.when((q >= 2) & ((z + 2) // nz == q))
        def _():
            zin_load(z + 2, lax.rem(z + 2, 3)).start()

        with jax.named_scope("wdwait"):
            wd_load(z, 0).wait()

        with jax.named_scope("zinwait"):
            @pl.when(q >= 2)
            def _():
                zin_load(z, lax.rem(z, 3)).wait()

        with jax.named_scope("zslot"):
            @pl.when(z >= Z_SLOTS)
            def _():
                z_send(z - Z_SLOTS).wait_send()

        with jax.named_scope("zmm"):
            acc = jnp.dot(hz[lax.rem(q, 2)], wdbuf[wslot], preferred_element_type=jnp.float32)
            zout[lax.rem(z, Z_SLOTS)] = acc + zinb[lax.rem(z, 3)]

        z_send(z).start()
        return carry

    def late(kind):
        base = nsum + (kind - 1) * nz
        h = 0 if kind < 3 else 1

        def tile(n, carry):
            w = base + n
            wd_fetch(w + 2)
            if kind == 2:
                z = nsum + n

                @pl.when(n + 2 < nz)
                def _():
                    zin_load(z + 2, lax.rem(n + 2, 3)).start()

            wd_load(w, kind).wait()
            if kind == 2:
                zin_load(z, lax.rem(n, 3)).wait()

                @pl.when(n >= 2)
                def _():
                    o_write(n - 2, lax.rem(n, 2)).wait()

            with jax.named_scope(f"late{kind}"):
                acc = jnp.dot(hz[h, :, wd_rows[kind]], wdbuf[lax.rem(w, WD_SLOTS), wd_rows[kind]], preferred_element_type=jnp.float32)
                if kind in (1, 3):
                    zacc[n] = acc
                elif kind == 2:
                    ofin[lax.rem(n, 2)] = (acc + zacc[n] + zinb[lax.rem(n, 3)]).astype(jnp.bfloat16)
                else:
                    zacc[n] += acc
            if kind == 2:
                o_write(n, lax.rem(n, 2)).start()
            if kind == 4:
                pltpu.make_async_copy(zacc.at[n], z_part.at[n], osem.at[2]).start()
            return carry

        with jax.named_scope("harr"):
            pull(jnp.int32(first_q + h), first_q + kind - 1, *spans[kind])
            if kind == 2:
                total(zin.at[0], zr.at[2 * RING - 4])
                for y in range(2):
                    zin_load(jnp.int32(nsum + y), y).start()
        with jax.named_scope("hzload"):
            pulled(first_q + h, *spans[kind])
        lax.fori_loop(0, nz, tile, 0)

    def z_done(g):
        q, k = jnp.maximum(g - zstart, 0), g - zstart - 2 * nt + 1
        steady = 2 * nz * (q // nt) + 2 * nz * (lax.rem(q, nt) + 1) // nt
        ending = 4 * nz + nz * k // 2
        return jnp.where(g < zstart, 0, jnp.where(k > 0, ending, steady))

    def body(g, carry):
        s, t = g // nt, lax.rem(g, nt)

        @pl.when(g == early - 1)
        def _():
            got_all(WN + 2, part_of(ws, 1))
            go(SW + 10, SW + 11)
            got(WL + 2)
            go(SW + 6)
            got(WF + 2)
            go(SW + 14)

        @pl.when(g == early)
        def _():
            got(WF + 3)
            go(SW + 15)
            got(WL + 3)
            go(SW + 7, YS + 2, YS + 3)

            def first(j, carry):
                serve(j, early)
                return carry

            lax.fori_loop(0, early, first, 0)
            got_all(SW + 2, wgu.at[:, :, pl.ds(p_dst[1], pc[1])])
            start_w(g)
            wd_load(0, 0).start()
            wd_load(1, 0).start()

        @pl.when(g < ng)
        def _():
            @pl.when((g + 1 < ng) & (g + 1 != early))
            def _():
                start_w(g + 1)

            @pl.when((t == nt - 1) & (g + 1 < ng))
            def _():
                @pl.when(s + 1 == 1)
                def _():
                    got_all(YF, xg.at[0])

                @pl.when(s + 1 == 2)
                def _():
                    got_all(YS, xg.at[0])

                for k in range(RING):
                    x_load(s + 1, k).start()

            with jax.named_scope("xwait"):
                @pl.when(t == 0)
                def _():
                    total(xbuf.at[lax.rem(s, 2)], xsem.at[lax.rem(s, 2)])

            with jax.named_scope("wwait"):
                total(wbuf.at[lax.rem(g, 2)], wsem.at[lax.rem(g, 2)])

            xslot, wslot, hslot = lax.rem(s, 2), lax.rem(g, 2), lax.rem(g, H_SLOTS)

            def part(h, carry):
                r = pl.ds(pl.multiple_of(h * part_rows, part_rows), part_rows)
                gu = jnp.dot(xbuf[xslot, r, :], wbuf[wslot], preferred_element_type=jnp.float32)
                gate = gu[:, :tn].astype(jnp.bfloat16).astype(jnp.float32)
                up = gu[:, tn:].astype(jnp.bfloat16).astype(jnp.float32)
                hout[hslot, h] = (jax.nn.silu(gate) * up).astype(jnp.bfloat16)
                return carry

            with jax.named_scope("gumm"):
                lax.fori_loop(0, 2, part, 0)
            h_write(g).start()

        @pl.when(g == 2 * nt)
        def _():
            all_sent()

        done, tiles = jnp.where(g == early, early, forwards(g - 1)), jnp.minimum(g + 1, ng)
        send(issued(done, jnp.minimum(g, ng)), issued(done, tiles))

        with jax.named_scope("fwd"):
            @pl.when(forwards(g) > done)
            def _():
                serve(done, tiles)

        @pl.when(g >= 1)
        def _():
            h_write(g - 1).wait()

        lax.fori_loop(z_done(g - 1), z_done(g), z_tile, 0)

        with jax.named_scope("fwd"):
            @pl.when(forwards(g) > done + 1)
            def _():
                serve(done + 1, tiles)

        return carry

    lax.fori_loop(0, ng, body, 0)

    tiles = jnp.int32(ng)

    def end_serve(j):
        with jax.named_scope("fwd"):
            serve(jnp.int32(j), tiles)

    lax.fori_loop(z_done(jnp.int32(ng - 1)), nsum, z_tile, 0)
    for j in range(ni - 2 * early, ni - 4):
        end_serve(j)
    h_write(ng - 1).wait()
    late(1)
    end_serve(ni - 4)
    late(2)
    end_serve(ni - 3)
    late(3)
    end_serve(ni - 2)
    end_serve(ni - 1)
    late(4)
    with jax.named_scope("harr"):
        total(hg.at[0, 0, :, pl.ds(ta, nt - ta)], hr.at[last_q + 3])
        total(zin.at[0], zr.at[2 * RING - 3])

    with jax.named_scope("drain"):
        for i in range(ni - 2, ni):
            total(hout.at[0], os.at[i % 8])
        for i in range(ni - 4, ni):
            h_fwd(jnp.int32(i)).wait_send()
        for z in range(max(0, nsum - Z_SLOTS), nsum):
            z_send(z).wait_send()
        for n in range(nz - 2, nz):
            o_write(jnp.int32(n), n % 2).wait()
        total(z_part, osem.at[2])


def _finish(hg, wd, zin, z_part, z_half, out, hz, wdb, zinb, accb, keep, res, hsem, wsem, zsem, asem, ksem, osem):
    rows, tn = hg.shape[4:]
    nz, _, zn = z_part.shape
    nt = hg.shape[3]
    ka = RING * tn * (nt - 2)
    b = lax.axis_index("dz")
    top, low = pl.ds(0, rows), pl.ds(rows, rows)

    for t in range(2):
        for k in range(RING):
            pltpu.make_async_copy(hg.at[b, k, 1, nt - 2 + t], hz.at[:, pl.ds((t * RING + k) * tn, tn)], hsem.at[0]).start()
    def cols(n):
        return pl.ds(pl.multiple_of(n * zn, 128), zn)

    def loads(n):
        return (
            pltpu.make_async_copy(wd.at[pl.ds(ka, 2 * RING * tn), cols(n)], wdb.at[n], wsem.at[n]),
            pltpu.make_async_copy(z_part.at[n], accb.at[n], asem.at[n]),
            pltpu.make_async_copy(zin.at[zin.shape[0] - 1, n], zinb.at[n], zsem.at[n]),
        )

    def fetch(n, carry):
        for copy in loads(n):
            copy.start()
        return carry

    lax.fori_loop(0, 2, fetch, 0)
    first = pltpu.make_async_copy(z_half, keep, ksem.at[0])
    pltpu.make_async_copy(hz, hz, hsem.at[0]).wait()

    def tile(n, carry):
        @pl.when(n + 2 < nz)
        def _():
            fetch(n + 2, 0)

        @pl.when(n == nz // 2)
        def _():
            first.start()

        for copy in loads(n):
            copy.wait()
        acc = jnp.dot(hz[...], wdb[n], preferred_element_type=jnp.float32)
        res[n] = (acc + accb[n] + zinb[n]).astype(jnp.bfloat16)
        pltpu.make_async_copy(res.at[n], out.at[low, cols(n)], osem.at[0]).start()
        return carry

    lax.fori_loop(0, nz - 1, tile, 0)
    first.wait()
    second = pltpu.make_async_copy(keep, out.at[top], ksem.at[1])
    second.start()
    lax.fori_loop(nz - 1, nz, tile, 0)
    pltpu.make_async_copy(out.at[low], out.at[low], osem.at[0]).wait()
    second.wait()


def _local(x_blk, wg_blk, wu_blk, wd_blk):
    rows, kb = x_blk.shape
    hc = wg_blk.shape[1] // RING
    mc = wd_blk.shape[1]
    tn, zn = _tile(2 * hc, 256), _tile(2 * mc, 256)
    nt, nz = 2 * hc // tn, 2 * mc // zn
    bf16, f32 = jnp.bfloat16, jnp.float32
    hbm = pl.BlockSpec(memory_space=pl.ANY)
    half = rows // 2
    dma = pltpu.SemaphoreType.DMA
    flops = 2 * RING * rows * (RING * kb * 4 * hc + wd_blk.shape[0] * 2 * mc)
    res = pl.pallas_call(
        _kernel,
        name="ring_mlp",
        out_shape=(
            jax.ShapeDtypeStruct((half, 2 * mc), bf16),
            jax.ShapeDtypeStruct((nz, half, zn), f32),
            jax.ShapeDtypeStruct((RING, RING, rows, kb), bf16),
            jax.ShapeDtypeStruct((2, RING * kb, 2 * hc), bf16),
            jax.ShapeDtypeStruct((2, kb, hc), bf16),
            jax.ShapeDtypeStruct((RING, RING, 2, nt, half, tn), bf16),
            jax.ShapeDtypeStruct(wd_blk.shape, bf16),
            jax.ShapeDtypeStruct((wd_blk.shape[0], 2 * mc), bf16),
            jax.ShapeDtypeStruct((2 * (RING - 1), nz, half, zn), f32),
        ),
        in_specs=[hbm] * 4,
        out_specs=(hbm,) * 9,
        scratch_shapes=[
            pltpu.VMEM((2, rows, RING * kb), bf16),
            pltpu.VMEM((2, RING * kb, 2 * tn), bf16),
            pltpu.VMEM((2, half, wd_blk.shape[0]), bf16),
            pltpu.VMEM((WD_SLOTS, wd_blk.shape[0], zn), bf16),
            pltpu.VMEM((3, half, zn), f32),
            pltpu.VMEM((Z_SLOTS, half, zn), f32),
            pltpu.VMEM((nz, half, zn), f32),
            pltpu.VMEM((2, half, zn), bf16),
            pltpu.VMEM((H_SLOTS, 2, half, tn), bf16),
            dma((5,)), dma((N_RECV,)), dma((3,)), dma((3,)),
            dma((2,)), dma((2,)), dma((1,)), dma((WD_SLOTS,)), dma((3,)), dma((3,)),
            dma((8,)), dma((2 * RING * nt,)), dma((8,)), dma((2 * RING + 3,)), dma((2,)),
            dma((Z_SLOTS,)), dma((2 * (RING - 1),)),
        ],
        compiler_params=pltpu.CompilerParams(collective_id=0, has_side_effects=True, vmem_limit_bytes=67043328),
        cost_estimate=pl.CostEstimate(flops=flops, bytes_accessed=flops // 500, transcendentals=0),
    )(x_blk, wg_blk, wu_blk, wd_blk)
    z_half, z_part, hg, wd, zin = res[0], res[1], res[5], res[7], res[8]
    flops = 2 * half * 2 * RING * tn * 2 * mc
    return pl.pallas_call(
        _finish,
        name="last_part",
        out_shape=jax.ShapeDtypeStruct((rows, 2 * mc), bf16),
        in_specs=[hbm] * 5,
        out_specs=hbm,
        scratch_shapes=[
            pltpu.VMEM((half, 2 * RING * tn), bf16),
            pltpu.VMEM((nz, 2 * RING * tn, zn), bf16),
            pltpu.VMEM((nz, half, zn), f32),
            pltpu.VMEM((nz, half, zn), f32),
            pltpu.VMEM((half, 2 * mc), bf16),
            pltpu.VMEM((nz, half, zn), bf16),
            dma((1,)), dma((nz,)), dma((nz,)), dma((nz,)), dma((2,)), dma((1,)),
        ],
        compiler_params=pltpu.CompilerParams(vmem_limit_bytes=67043328),
        cost_estimate=pl.CostEstimate(flops=flops, bytes_accessed=flops // 500, transcendentals=0),
    )(hg, wd, zin, z_part, z_half)


def solution(mesh):
    assert mesh.shape["dz"] == RING and mesh.shape["dy"] == RING and mesh.shape["dx"] == 2
    x_spec = P(("grp", "dx", "dz"), "dy")
    w_in_spec = P("dy", ("dz", "dx"))
    w_out_spec = P("dz", ("dy", "dx"))
    return jax.shard_map(_local, mesh=mesh, in_specs=(x_spec, w_in_spec, w_in_spec, w_out_spec), out_specs=x_spec, check_vma=False)
```

profile of v0, /device:TPU:97, one launch (start us, length us, event | category | flops | bytes accessed | tf_op | source)
XLA Modules:
  0.0 558.5 jit_solution(11289516419986578124)
XLA Ops:
  0.0 550.3 %ring_mlp.1 = (bf16[384,1792]{1,0:T(8,128)(2,1)}, f32[7,384,256]{2,1,0:T(8,128)}, bf16[4,4,768,1792]{3,2,1,0:T(8,128)(2,1)}, bf16[2,7168,1280]{2,1,0:T(8,128)(2,...) custom-call(bf16[768,1792]{1,0:T(8,128)(2,1)} %x_in.1, ...), custom_call_target="tpu_custom_call" | custom-call | flops 169114337280 | bytes 338228672 | tf_op jit(solution)/shard_map/ring_mlp/pallas_call | solution.py:659
  550.3 8.2 %last_part.1 = bf16[768,1792]{1,0:T(8,128)(2,1)} custom-call(bf16[4,4,2,5,384,256]{5,4,3,2,1,0:T(8,128)(2,1)} %get-tuple-element.10.hg, bf16[5120,1792]{1,0:T(8,128)(2,1)} %get-tuple-element.11.wd, f32[6,7,384,256]{3,2,1,0:T(8,128)} %get-tuple-element.12.zin, f32[7,384,256]{2,1,0:T(8,128)} %get-tuple-element.13.z_part, ...), custom_call_target="tpu_custom_call" | custom-call | flops 2818572288 | bytes 5637144 | tf_op jit(solution)/shard_map/last_part/pallas_call | solution.py:695
where the time goes:
time: 559 us; the launch traced here: 558 us
  Pallas kernels  558 us (100%)
    pallas_call x1, Pallas kernels, _local(): pl.pallas_call(_kernel, name='ring_mlp', out_shape=(jax.ShapeDtypeStruct(...  550 us

commit v1 on v0

--- a/solution.py
+++ b/solution.py
@@ -616,19 +616,12 @@
             copy.start()
         return carry
 
-    lax.fori_loop(0, 2, fetch, 0)
+    lax.fori_loop(0, nz, fetch, 0)
     first = pltpu.make_async_copy(z_half, keep, ksem.at[0])
+    first.start()
     pltpu.make_async_copy(hz, hz, hsem.at[0]).wait()
 
     def tile(n, carry):
-        @pl.when(n + 2 < nz)
-        def _():
-            fetch(n + 2, 0)
-
-        @pl.when(n == nz // 2)
-        def _():
-            first.start()
-
         for copy in loads(n):
             copy.wait()
         acc = jnp.dot(hz[...], wdb[n], preferred_element_type=jnp.float32)

time: 559 us -> 558 us (level)
  no operation moved by 1% of the time
where the time goes in v1:
time: 558 us
  Pallas kernels  558 us (100%)
    pallas_call x1, Pallas kernels, _local(): pl.pallas_call(_kernel, name='ring_mlp', out_shape=(jax.ShapeDtypeStruct(...  550 us

profile of v1, /device:TPU:97, one launch (start us, length us, event | category | flops | bytes accessed | tf_op | source)
XLA Modules:
  0.0 557.9 jit_solution(16630411353163526029)
XLA Ops:
  0.0 550.3 %ring_mlp.1 = (bf16[384,1792]{1,0:T(8,128)(2,1)}, f32[7,384,256]{2,1,0:T(8,128)}, bf16[4,4,768,1792]{3,2,1,0:T(8,128)(2,1)}, bf16[2,7168,1280]{2,1,0:T(8,128)(2,...) custom-call(bf16[768,1792]{1,0:T(8,128)(2,1)} %x_in.1, ...), custom_call_target="tpu_custom_call" | custom-call | flops 169114337280 | bytes 338228672 | tf_op jit(solution)/shard_map/ring_mlp/pallas_call | solution.py:652
  550.3 7.6 %last_part.1 = bf16[768,1792]{1,0:T(8,128)(2,1)} custom-call(bf16[4,4,2,5,384,256]{5,4,3,2,1,0:T(8,128)(2,1)} %get-tuple-element.10.hg, bf16[5120,1792]{1,0:T(8,128)(2,1)} %get-tuple-element.11.wd, f32[6,7,384,256]{3,2,1,0:T(8,128)} %get-tuple-element.12.zin, f32[7,384,256]{2,1,0:T(8,128)} %get-tuple-element.13.z_part, ...), custom_call_target="tpu_custom_call" | custom-call | flops 2818572288 | bytes 5637144 | tf_op jit(solution)/shard_map/last_part/pallas_call | solution.py:688

commit v2 on v1

--- a/solution.py
+++ b/solution.py
@@ -574,10 +574,6 @@
     end_serve(ni - 2)
     end_serve(ni - 1)
     late(4)
-    with jax.named_scope("harr"):
-        total(hg.at[0, 0, :, pl.ds(ta, nt - ta)], hr.at[last_q + 3])
-        total(zin.at[0], zr.at[2 * RING - 3])
-
     with jax.named_scope("drain"):
         for i in range(ni - 2, ni):
             total(hout.at[0], os.at[i % 8])
@@ -587,6 +583,10 @@
             z_send(z).wait_send()
         for n in range(nz - 2, nz):
             o_write(jnp.int32(n), n % 2).wait()
+
+    with jax.named_scope("harr"):
+        total(hg.at[0, 0, :, pl.ds(ta, nt - ta)], hr.at[last_q + 3])
+        total(zin.at[0], zr.at[2 * RING - 3])
         total(z_part, osem.at[2])
 
 

time: 558 us -> 558 us (level)
  no operation moved by 1% of the time
where the time goes in v2:
time: 558 us
  Pallas kernels  558 us (100%)
    pallas_call x1, Pallas kernels, _local(): pl.pallas_call(_kernel, name='ring_mlp', out_shape=(jax.ShapeDtypeStruct(...  550 us

profile of v2, /device:TPU:97, one launch (start us, length us, event | category | flops | bytes accessed | tf_op | source)
XLA Modules:
  0.0 557.9 jit_solution(3724370227087390507)
XLA Ops:
  0.0 550.3 %ring_mlp.1 = (bf16[384,1792]{1,0:T(8,128)(2,1)}, f32[7,384,256]{2,1,0:T(8,128)}, bf16[4,4,768,1792]{3,2,1,0:T(8,128)(2,1)}, bf16[2,7168,1280]{2,1,0:T(8,128)(2,...) custom-call(bf16[768,1792]{1,0:T(8,128)(2,1)} %x_in.1, ...), custom_call_target="tpu_custom_call" | custom-call | flops 169114337280 | bytes 338228672 | tf_op jit(solution)/shard_map/ring_mlp/pallas_call | solution.py:652
  550.3 7.6 %last_part.1 = bf16[768,1792]{1,0:T(8,128)(2,1)} custom-call(bf16[4,4,2,5,384,256]{5,4,3,2,1,0:T(8,128)(2,1)} %get-tuple-element.10.hg, bf16[5120,1792]{1,0:T(8,128)(2,1)} %get-tuple-element.11.wd, f32[6,7,384,256]{3,2,1,0:T(8,128)} %get-tuple-element.12.zin, f32[7,384,256]{2,1,0:T(8,128)} %get-tuple-element.13.z_part, ...), custom_call_target="tpu_custom_call" | custom-call | flops 2818572288 | bytes 5637144 | tf_op jit(solution)/shard_map/last_part/pallas_call | solution.py:688
